TPU v7x, 32 devices: a whole 2x2x4 slice. The times are simulated.
32 devices in a mesh: param: 16 (over z, y, x), sensor: 2 (over core).
Axes of the slice: x: 2, y: 2, z: 4, core: 2. Of those that a mesh axis runs over, the one named last changes fastest.
Arguments:
- data: float32 [16, 512, 420], P(None, ('sensor', 'param')), may hold values from -6 to 6
- spectra: float32 [2, 512, 64, 421], P(None, 'sensor', 'param'), may hold values from -2 to 2
Outputs:
- gradient: float32 [16, 64, 420], P(None, 'param')
- rms: float32 [16], replicated
All inputs are finite; a program needn't handle non-finite values.
Results may differ from a plain program's by a relative error of at most 0.0003.
Values sent between devices are 32-bit elements; how exact they have to be, the bound alone decides.
A program may use at most 128 MiB of HBM per device.

v0:
```python
import math
import jax
import jax.numpy as jnp
from jax import lax
from jax.sharding import PartitionSpec as P


def spectral_tables(steps):
    length = 2 * steps
    freqs = steps + 1
    times = lax.broadcasted_iota(jnp.int32, (steps, freqs), 0)
    bins = lax.broadcasted_iota(jnp.int32, (steps, freqs), 1)
    phase = 2.0 * math.pi / length * (times * bins % length).astype(jnp.float32)
    forward = jnp.concatenate([jnp.cos(phase), -jnp.sin(phase)], axis=1)
    weight = jnp.where((bins == 0) | (bins == steps), 1.0, 2.0) / length
    backward = jnp.concatenate([(weight * jnp.cos(phase)).T, (-weight * jnp.sin(phase)).T], axis=0)
    return (forward, backward)


def to_spectrum(series, forward):
    vectors, sensors, steps = series.shape
    flat = jnp.dot(
        series.reshape(vectors * sensors, steps),
        forward,
        precision=lax.Precision.HIGHEST,
        preferred_element_type=jnp.float32,
    )
    return flat.reshape(vectors, sensors, forward.shape[1])


def contract(kernel, spectrum):
    return jnp.einsum(
        "spf,rsf->rpf",
        kernel,
        spectrum,
        precision=lax.Precision.HIGHEST,
        preferred_element_type=jnp.float32,
    )


def body(data, spectra):
    steps = data.shape[2]
    freqs = steps + 1
    forward, backward = spectral_tables(steps)
    whole = to_spectrum(lax.all_gather(data, "param", axis=1, tiled=True), forward)
    real_part = whole[..., :freqs]
    imag_part = whole[..., freqs:]
    kernel_re = spectra[0]
    kernel_im = spectra[1]
    out_re = contract(kernel_re, real_part) + contract(kernel_im, imag_part)
    out_im = contract(kernel_re, imag_part) - contract(kernel_im, real_part)
    vectors, points = (out_re.shape[0], out_re.shape[1])
    stacked = jnp.concatenate([out_re, out_im], axis=2).reshape(vectors * points, 2 * freqs)
    partial_field = jnp.dot(
        stacked, backward, precision=lax.Precision.HIGHEST, preferred_element_type=jnp.float32
    ).reshape(vectors, points, steps)
    count = points * lax.axis_size("param") * steps
    share = lax.psum_scatter(partial_field, "sensor", scatter_dimension=0, tiled=True)
    squares = lax.psum(jnp.sum(share * share, axis=(1, 2)), "param")
    scale = jnp.sqrt(squares / count + 1e-06)
    normalized = share / scale[:, None, None]
    gradient, rms_all = (
        lax.all_gather(normalized, "sensor", axis=0, tiled=True),
        lax.all_gather(scale, "sensor", axis=0, tiled=True),
    )
    return (gradient, rms_all)


def solution(mesh):
    in_specs = (P(None, ("sensor", "param"), None), P(None, "sensor", "param", None))
    out_specs = (P(None, "param", None), P())
    return jax.shard_map(body, mesh=mesh, in_specs=in_specs, out_specs=out_specs, check_vma=False)
```

profile of v0, /device:TPU:0, one launch (start us, length us, event | category | flops | bytes accessed | tf_op | source)
XLA Modules:
  0.0 326.7 jit_solution(8645191133042081712)
XLA Ops:
  7.2 0.0 copy-start
  7.2 0.0 all-gather.2.cloned.1.call-start
  7.2 0.7 all-gather.2.cloned.1.call-update
  7.9 0.0 reduce-scatter.2.cloned.1.call-start
  8.0 4.5 %sine_negate_fusion = (f32[420,421]{1,0:T(8,128)}, f32[420,421]{1,0:T(8,128)}) fusion(), kind=kLoop, calls=%fused_computation.39 | loop fusion | flops 1768200 | bytes 1414560 | tf_op jit(solution)/shard_map/neg | solution.py:14
  12.5 4.6 %sine_multiply_fusion = (f32[421,420]{0,1:T(8,128)}, f32[421,420]{0,1:T(8,128)}) fusion(f32[421]{0:T(512)S(1)} %fusion.42, f32[421]{0:T(512)S(1)} %select_multiply_fusion), kind=kLoop, calls=%fused_computation.34 | loop fusion | flops 1945020 | bytes 1417928 | tf_op jit(solution)/shard_map/mul | solution.py:16
  17.0 0.0 copy-done
  17.0 1.5 fusion.73
  18.5 1.5 fusion.71
  20.0 1.5 fusion.75
  21.6 1.5 fusion.77
  23.1 102.6 %all-gather.2.cloned.1.call-done = f32[16,256,420]{2,1,0:T(8,128)} async-done(((f32[16,16,420]{2,1,0:T(8,128)}), f32[16,256,420]{2,1,0:T(8,128)}) %all-gather.2.cloned.1.call-update) | async-done | bytes 6881296 | tf_op jit(solution)/shard_map/all_gather | solution.py:45
  125.7 51.7 %fusion.20 = f32[842,4096]{1,0:T(8,128)} fusion(f32[4096,420]{1,0:T(8,128)} %bitcast.71, f32[420,421]{1,0:T(8,128)} %get-tuple-element.6, f32[420,421]{1,0:T(8,128)} %get-tuple-element.7), kind=kOutput, calls=%fused_computation.20 | convolution fusion | flops 17382467584 | bytes 22091168 | tf_op jit(solution)/shard_map/dot_general | solution.py:22
  177.4 0.0 copy-start.4
  177.4 16.8 %copy.9 = f32[106,8,16,256]{3,2,1,0:T(8,128)} copy(f32[106,8,16,256]{3,1,2,0:T(8,128)} %bitcast.70) | data formatting | bytes 27787264
  194.2 0.0 copy-done.4
  194.2 0.0 copy-start.3
  194.2 14.2 %fusion.2 = f32[421,16,4]{1,2,0:T(4,128)} fusion(f32[848,16,256]{2,1,0:T(8,128)} %bitcast.66, f32[256,4,421]{0,1,2:T(4,128)S(1)} %copy-done.4), kind=kOutput, calls=%fused_computation.2 | convolution fusion | flops 82771968 | bytes 15627520 | tf_op jit(solution)/shard_map/spf,rsf->rpf/dot_general | solution.py:32
  208.5 2.1 copy.5
  210.6 0.0 copy-done.3
  210.6 0.0 copy-start.2
  210.6 14.2 %fusion = f32[421,16,4]{1,2,0:T(4,128)} fusion(f32[848,16,256]{2,1,0:T(8,128)} %bitcast.67, f32[256,4,421]{0,1,2:T(4,128)S(1)} %copy-done.3), kind=kOutput, calls=%fused_computation | convolution fusion | flops 82771968 | bytes 15627520 | tf_op jit(solution)/shard_map/spf,rsf->rpf/dot_general | solution.py:32
  224.8 2.1 copy.6
  226.9 0.0 copy-done.2
  226.9 0.0 copy-start.1
  226.9 14.3 %fusion.4 = f32[421,16,4]{1,2,0:T(4,128)} fusion(f32[848,16,256]{2,1,0:T(8,128)} %bitcast.68, f32[256,4,421]{0,1,2:T(4,128)S(1)} %copy-done.2), kind=kOutput, calls=%fused_computation.4 | convolution fusion | flops 82771968 | bytes 15627520 | tf_op jit(solution)/shard_map/spf,rsf->rpf/dot_general | solution.py:32
  241.2 2.1 copy.7
  243.3 0.0 copy-done.1
  243.3 0.0 copy-start.5
  243.3 0.0 copy-start.6
  243.3 14.1 %fusion.6 = f32[421,16,4]{1,2,0:T(4,128)} fusion(f32[848,16,256]{2,1,0:T(8,128)} %bitcast.69, f32[256,4,421]{0,1,2:T(4,128)S(1)} %copy-done.1), kind=kOutput, calls=%fused_computation.6 | convolution fusion | flops 82771968 | bytes 15627520 | tf_op jit(solution)/shard_map/spf,rsf->rpf/dot_general | solution.py:32
  257.4 0.0 copy-start.7
  257.4 1.5 copy.8
  258.9 1.0 add_bitcast_fusion
  259.9 0.9 subtract_bitcast_fusion
  260.8 0.0 copy-done.5
  260.8 0.0 copy-done.6
  260.8 2.3 fusion.24
  263.1 0.0 reduce-scatter.2.cloned.1.call-update
  263.1 0.0 copy-done.7
  263.1 0.6 dynamic-slice
  263.7 5.8 %reduce-scatter.2.cloned.1.call-done = f32[8,4,420]{2,0,1:T(8,128)} async-done(((f32[16,4,420]{2,0,1:T(8,128)}), f32[8,4,420]{2,0,1:T(8,128)}) %reduce-scatter.2.cloned.1.call-update) | async-done | bytes 53776 | tf_op jit(solution)/shard_map/reduce_scatter | solution.py:58
  269.5 1.0 multiply_reduce_fusion
  271.1 41.9 %psum.7 = f32[8]{0:T(128)S(1)} all-reduce(f32[8]{0:T(128)S(1)} %multiply_reduce_fusion), channel_id=1, replica_groups=mesh['param'=16,'sensor'=2] {'param'}, use_global_device_ids=true, to_apply=%region_2.3 | all-reduce | flops 8 | bytes 64 | tf_op jit(solution)/shard_map/psum | solution.py:59
  313.0 0.1 fusion.45
  313.1 0.9 broadcast_divide_fusion
  314.0 1.9 all_gather.10
  315.9 0.7 copy.4
  316.7 2.9 all-reduce
  (3 shorter events, 0.0 us)
Async XLA Ops:
  7.2 9.9 %copy-start = (f32[2,256,4,421]{1,2,3,0:T(4,128)S(1)}, f32[2,256,4,421]{1,2,3,0:T(4,128)}, u32[]{:S(2)}) copy-start(f32[2,256,4,421]{1,2,3,0:T(4,128)} %param.3) | copy-start | bytes 10346500
  7.2 118.6 %all-gather.2.cloned.1.call-start = ((), (), s32[]{:S(2)}) async-start(), calls=%async_computation.1 | async-start | bytes 8912896 | tf_op jit(solution)/shard_map/all_gather | solution.py:45
  7.9 261.6 %reduce-scatter.2.cloned.1.call-start = ((), (), s32[]{:S(2)}) async-start(), calls=%async_computation.2 | async-start | bytes 196608 | tf_op jit(solution)/shard_map/reduce_scatter | solution.py:58
  177.4 16.8 %copy-start.4 = (f32[256,4,421]{0,1,2:T(4,128)S(1)}, f32[256,4,421]{0,1,2:T(4,128)}, u32[]{:S(2)}) copy-start(f32[256,4,421]{0,1,2:T(4,128)} %fusion.73) | copy-start | bytes 5173252
  194.2 16.3 %copy-start.3 = (f32[256,4,421]{0,1,2:T(4,128)S(1)}, f32[256,4,421]{0,1,2:T(4,128)}, u32[]{:S(2)}) copy-start(f32[256,4,421]{0,1,2:T(4,128)} %fusion.71) | copy-start | bytes 5173252
  210.6 16.3 %copy-start.2 = (f32[256,4,421]{0,1,2:T(4,128)S(1)}, f32[256,4,421]{0,1,2:T(4,128)}, u32[]{:S(2)}) copy-start(f32[256,4,421]{0,1,2:T(4,128)} %fusion.75) | copy-start | bytes 5173252
  226.9 16.4 %copy-start.1 = (f32[256,4,421]{0,1,2:T(4,128)S(1)}, f32[256,4,421]{0,1,2:T(4,128)}, u32[]{:S(2)}) copy-start(f32[256,4,421]{0,1,2:T(4,128)} %fusion.77) | copy-start | bytes 5173252
  243.3 17.5 %copy-start.5 = (f32[421,420]{0,1:T(8,128)S(1)}, f32[421,420]{0,1:T(8,128)}, u32[]{:S(2)}) copy-start(f32[421,420]{0,1:T(8,128)} %get-tuple-element.8) | copy-start | bytes 2121844
  243.3 17.5 %copy-start.6 = (f32[421,420]{0,1:T(8,128)S(1)}, f32[421,420]{0,1:T(8,128)}, u32[]{:S(2)}) copy-start(f32[421,420]{0,1:T(8,128)} %get-tuple-element.9) | copy-start | bytes 2121844
  257.4 5.7 %copy-start.7 = (u32[32]{0:T(128)S(1)}, u32[32]{0:T(128)}, u32[]{:S(2)}) copy-start(u32[32]{0:T(128)} %constant.35) | copy-start | bytes 388
Sparse Core Ops, SparseCore 0:
  10.8 114.9 all-gather.1
  263.2 6.2 reduce-scatter.1
where the time goes:
time: 330 us; the launch traced here: 327 us
  matrix products  111 us (34%)
  waiting for transfers between devices  109 us (33%)
  blocking collectives  46.8 us (14%)
  local copies, waits for them, and re-layouts  32 us (10%)
  between operations  15 us (5%)
  other arithmetic  13 us (4%)
    all_gather x1, waiting for transfers between devices, body(): lax.all_gather(data, 'param', axis=1, tiled=True)  103 us
    dot_general x4, matrix products, contract(): jnp.einsum('spf,rsf->rpf', kernel, spectrum, precision=lax.Precision.HIGH...  56.8 us
    dot_general x1, matrix products, to_spectrum(): jnp.dot(series.reshape(vectors * sensors, steps), forward, precision=lax....  51.7 us
    psum x1, blocking collectives, body(): squares = lax.psum(jnp.sum(share * share, axis=(1, 2)), 'param')  41.9 us
    unnamed x20, local copies, waits for them, and re-layouts  18.2 us
    dot_general x8, local copies, waits for them, and re-layouts, contract(): jnp.einsum('spf,rsf->rpf', kernel, spectrum, precision=lax.Precision.HIGH...  13.8 us
  transfers between devices with their start and end apart: 2, of which 2 were waited for; matrix products, arithmetic and copies ran while one was open for 5% of the time, Pallas kernels for 0%

commit v1 on v0

--- a/solution.py
+++ b/solution.py
@@ -56,7 +56,9 @@
     ).reshape(vectors, points, steps)
     count = points * lax.axis_size("param") * steps
     share = lax.psum_scatter(partial_field, "sensor", scatter_dimension=0, tiled=True)
-    squares = lax.psum(jnp.sum(share * share, axis=(1, 2)), "param")
+    part = jnp.sum(share * share, axis=(1, 2))
+    parts = lax.all_gather(part, "param")
+    squares = jnp.sum(parts, axis=0)
     scale = jnp.sqrt(squares / count + 1e-06)
     normalized = share / scale[:, None, None]
     gradient, rms_all = (

time: 330 us -> 330 us (level)
    psum x1 -> x0, blocking collectives: 41.9 us -> none  [body(): squares = lax.psum(jnp.sum(share * share, axis=(1, 2)), 'param')]
    unnamed x1 -> x2, blocking collectives: 2.95 us -> 44.8 us
    unnamed x20 -> x25, local copies, waits for them, and re-layouts: 18.2 us -> 19 us
where the time goes in v1:
time: 330 us; the launch traced here: 327 us
  matrix products  111 us (34%)
  waiting for transfers between devices  107 us (32%)
  blocking collectives  46.7 us (14%)
  local copies, waits for them, and re-layouts  32.9 us (10%)
  between operations  15.6 us (5%)
  other arithmetic  13 us (4%)
    all_gather x1, waiting for transfers between devices, body(): lax.all_gather(data, 'param', axis=1, tiled=True)  103 us
    dot_general x4, matrix products, contract(): jnp.einsum('spf,rsf->rpf', kernel, spectrum, precision=lax.Precision.HIGH...  57.1 us
    dot_general x1, matrix products, to_spectrum(): jnp.dot(series.reshape(vectors * sensors, steps), forward, precision=lax....  51.8 us
    unnamed x2, blocking collectives  44.8 us
    unnamed x25, local copies, waits for them, and re-layouts  19 us
    dot_general x8, local copies, waits for them, and re-layouts, contract(): jnp.einsum('spf,rsf->rpf', kernel, spectrum, precision=lax.Precision.HIGH...  13.9 us
  transfers between devices with their start and end apart: 2, of which 2 were waited for; matrix products, arithmetic and copies ran while one was open for 5% of the time, Pallas kernels for 0%

profile of v1, /device:TPU:0, one launch (start us, length us, event | category | flops | bytes accessed | tf_op | source)
XLA Modules:
  0.0 326.8 jit_solution(10763029362317359491)
XLA Ops:
  7.2 0.0 copy-start
  7.2 0.0 all-gather.3.cloned.1.call-start
  7.2 0.7 all-gather.3.cloned.1.call-update
  7.9 0.0 reduce-scatter.2.cloned.1.call-start
  8.0 4.5 %sine_negate_fusion = (f32[420,421]{1,0:T(8,128)}, f32[420,421]{1,0:T(8,128)}) fusion(), kind=kLoop, calls=%fused_computation.39 | loop fusion | flops 1768200 | bytes 1414560 | tf_op jit(solution)/shard_map/neg | solution.py:14
  12.5 4.6 %sine_multiply_fusion = (f32[421,420]{0,1:T(8,128)}, f32[421,420]{0,1:T(8,128)}) fusion(f32[421]{0:T(512)S(1)} %fusion.42, f32[421]{0:T(512)S(1)} %select_multiply_fusion), kind=kLoop, calls=%fused_computation.34 | loop fusion | flops 1945020 | bytes 1417928 | tf_op jit(solution)/shard_map/mul | solution.py:16
  17.1 0.0 copy-done
  17.1 1.5 fusion.73
  18.6 1.5 fusion.71
  20.1 1.5 fusion.75
  21.6 1.5 fusion.77
  23.1 102.6 %all-gather.3.cloned.1.call-done = f32[16,256,420]{2,1,0:T(8,128)} async-done(((f32[16,16,420]{2,1,0:T(8,128)}), f32[16,256,420]{2,1,0:T(8,128)}) %all-gather.3.cloned.1.call-update) | async-done | bytes 6881296 | tf_op jit(solution)/shard_map/all_gather | solution.py:45
  125.7 51.8 %fusion.20 = f32[842,4096]{1,0:T(8,128)} fusion(f32[4096,420]{1,0:T(8,128)} %bitcast.72, f32[420,421]{1,0:T(8,128)} %get-tuple-element.8, f32[420,421]{1,0:T(8,128)} %get-tuple-element.9), kind=kOutput, calls=%fused_computation.20 | convolution fusion | flops 17382467584 | bytes 22091168 | tf_op jit(solution)/shard_map/dot_general | solution.py:22
  177.5 0.0 copy-start.4
  177.5 16.8 %copy.10 = f32[106,8,16,256]{3,2,1,0:T(8,128)} copy(f32[106,8,16,256]{3,1,2,0:T(8,128)} %bitcast.71) | data formatting | bytes 27787264
  194.3 0.0 copy-done.4
  194.3 0.0 copy-start.3
  194.3 14.2 %fusion.2 = f32[421,16,4]{1,2,0:T(4,128)} fusion(f32[848,16,256]{2,1,0:T(8,128)} %bitcast.67, f32[256,4,421]{0,1,2:T(4,128)S(1)} %copy-done.4), kind=kOutput, calls=%fused_computation.2 | convolution fusion | flops 82771968 | bytes 15627520 | tf_op jit(solution)/shard_map/spf,rsf->rpf/dot_general | solution.py:32
  208.6 2.1 copy.6
  210.7 0.0 copy-done.3
  210.7 0.0 copy-start.2
  210.7 14.2 %fusion = f32[421,16,4]{1,2,0:T(4,128)} fusion(f32[848,16,256]{2,1,0:T(8,128)} %bitcast.68, f32[256,4,421]{0,1,2:T(4,128)S(1)} %copy-done.3), kind=kOutput, calls=%fused_computation | convolution fusion | flops 82771968 | bytes 15627520 | tf_op jit(solution)/shard_map/spf,rsf->rpf/dot_general | solution.py:32
  224.9 2.1 copy.7
  227.0 0.0 copy-done.2
  227.0 0.0 copy-start.1
  227.0 14.3 %fusion.4 = f32[421,16,4]{1,2,0:T(4,128)} fusion(f32[848,16,256]{2,1,0:T(8,128)} %bitcast.69, f32[256,4,421]{0,1,2:T(4,128)S(1)} %copy-done.2), kind=kOutput, calls=%fused_computation.4 | convolution fusion | flops 82771968 | bytes 15627520 | tf_op jit(solution)/shard_map/spf,rsf->rpf/dot_general | solution.py:32
  241.3 2.1 copy.8
  243.4 0.0 copy-done.1
  243.4 0.0 copy-start.5
  243.4 0.0 copy-start.6
  243.4 14.3 %fusion.6 = f32[421,16,4]{1,2,0:T(4,128)} fusion(f32[848,16,256]{2,1,0:T(8,128)} %bitcast.70, f32[256,4,421]{0,1,2:T(4,128)S(1)} %copy-done.1), kind=kOutput, calls=%fused_computation.6 | convolution fusion | flops 82771968 | bytes 15627520 | tf_op jit(solution)/shard_map/spf,rsf->rpf/dot_general | solution.py:32
  257.8 0.0 copy-start.8
  257.8 0.0 copy-start.7
  257.8 1.5 copy.9
  259.3 1.0 add_bitcast_fusion
  260.3 0.9 subtract_bitcast_fusion
  261.2 0.0 copy-done.5
  261.2 0.0 copy-done.6
  261.2 2.3 fusion.24
  263.5 0.0 reduce-scatter.2.cloned.1.call-update
  263.5 0.0 copy-done.8
  263.5 0.6 dynamic-slice
  264.1 0.0 copy-done.7
  264.1 0.6 dynamic-slice.1
  265.9 4.0 %reduce-scatter.2.cloned.1.call-done = f32[8,4,420]{2,0,1:T(8,128)} async-done(((f32[16,4,420]{2,0,1:T(8,128)}), f32[8,4,420]{2,0,1:T(8,128)}) %reduce-scatter.2.cloned.1.call-update) | async-done | bytes 53776 | tf_op jit(solution)/shard_map/reduce_scatter | solution.py:58
  269.9 1.0 multiply_reduce_fusion
  270.9 0.2 dynamic-update-slice
  271.1 41.9 %all-reduce = f32[128]{0:T(128)S(1)} all-reduce(f32[128]{0:T(128)S(1)} %dynamic-update-slice), channel_id=2, replica_groups=mesh['param'=16,'sensor'=2] {'param'}, use_global_device_ids=true, to_apply=%add | all-reduce | flops 128 | bytes 1024
  313.0 0.1 reshape.21
  313.1 0.1 fusion.45
  313.2 0.9 broadcast_divide_fusion
  314.1 1.9 all_gather.18
  316.0 0.7 copy.5
  316.8 2.9 all-reduce.1
  (5 shorter events, 0.0 us)
Async XLA Ops:
  7.2 9.9 %copy-start = (f32[2,256,4,421]{1,2,3,0:T(4,128)S(1)}, f32[2,256,4,421]{1,2,3,0:T(4,128)}, u32[]{:S(2)}) copy-start(f32[2,256,4,421]{1,2,3,0:T(4,128)} %param.3) | copy-start | bytes 10346500
  7.2 118.6 %all-gather.3.cloned.1.call-start = ((), (), s32[]{:S(2)}) async-start(), calls=%async_computation.1 | async-start | bytes 8912896 | tf_op jit(solution)/shard_map/all_gather | solution.py:45
  7.9 262.0 %reduce-scatter.2.cloned.1.call-start = ((), (), s32[]{:S(2)}) async-start(), calls=%async_computation.2 | async-start | bytes 196608 | tf_op jit(solution)/shard_map/reduce_scatter | solution.py:58
  177.5 16.8 %copy-start.4 = (f32[256,4,421]{0,1,2:T(4,128)S(1)}, f32[256,4,421]{0,1,2:T(4,128)}, u32[]{:S(2)}) copy-start(f32[256,4,421]{0,1,2:T(4,128)} %fusion.73) | copy-start | bytes 5173252
  194.3 16.3 %copy-start.3 = (f32[256,4,421]{0,1,2:T(4,128)S(1)}, f32[256,4,421]{0,1,2:T(4,128)}, u32[]{:S(2)}) copy-start(f32[256,4,421]{0,1,2:T(4,128)} %fusion.71) | copy-start | bytes 5173252
  210.7 16.3 %copy-start.2 = (f32[256,4,421]{0,1,2:T(4,128)S(1)}, f32[256,4,421]{0,1,2:T(4,128)}, u32[]{:S(2)}) copy-start(f32[256,4,421]{0,1,2:T(4,128)} %fusion.75) | copy-start | bytes 5173252
  227.0 16.4 %copy-start.1 = (f32[256,4,421]{0,1,2:T(4,128)S(1)}, f32[256,4,421]{0,1,2:T(4,128)}, u32[]{:S(2)}) copy-start(f32[256,4,421]{0,1,2:T(4,128)} %fusion.77) | copy-start | bytes 5173252
  243.4 17.8 %copy-start.5 = (f32[421,420]{0,1:T(8,128)S(1)}, f32[421,420]{0,1:T(8,128)}, u32[]{:S(2)}) copy-start(f32[421,420]{0,1:T(8,128)} %get-tuple-element.10) | copy-start | bytes 2121844
  243.4 17.8 %copy-start.6 = (f32[421,420]{0,1:T(8,128)S(1)}, f32[421,420]{0,1:T(8,128)}, u32[]{:S(2)}) copy-start(f32[421,420]{0,1:T(8,128)} %get-tuple-element.11) | copy-start | bytes 2121844
  257.8 5.7 %copy-start.8 = (u32[32]{0:T(128)S(1)}, u32[32]{0:T(128)}, u32[]{:S(2)}) copy-start(u32[32]{0:T(128)} %constant.35) | copy-start | bytes 388
  257.8 6.3 %copy-start.7 = (u32[32]{0:T(128)S(1)}, u32[32]{0:T(128)}, u32[]{:S(2)}) copy-start(u32[32]{0:T(128)} %constant.40) | copy-start | bytes 388
Sparse Core Ops, SparseCore 0:
  10.8 114.9 all-gather.2
  263.6 6.2 reduce-scatter.1
